TPU v7x, 32 devices: a whole 2x2x4 slice. The times are simulated.
32 devices in a mesh: grid: 8 (over y, x, core), atom: 4 (over z).
Axes of the slice: x: 2, y: 2, z: 4, core: 2. Of those that a mesh axis runs over, the one named last changes fastest.
Arguments:
- basis_values: bfloat16 [64, 128, 512], P(('grid', 'atom')), may hold values from -8 to 8
- block_lists: int32 [64, 4], P('grid'), may hold values from 0 to 95, as said below
- orbitals: bfloat16 [12288, 4096], P('grid', 'atom'), may hold values from -0.00390625 to 0.00390625
- point_weights: float32 [8192], P(('grid', 'atom')), may hold values from 0.1 to 1
- point_atoms: int32 [8192], P(('grid', 'atom')), may hold values from 0 to 127, as said below
- embed_scale: float32 [256], replicated, may hold values from -4 to 4
- embed_shift: float32 [256], replicated, may hold values from -3 to 3
- message_weight: bfloat16 [2, 256, 256], replicated, may hold values from -0.375 to 0.375
- atom_weight: bfloat16 [2, 256, 256], replicated, may hold values from -0.375 to 0.375
- head_weight: float32 [256], replicated, may hold values from -0.375 to 0.375
Outputs:
- fock_orbitals: float32 [12288, 4096], P('grid', 'atom')
- potential: float32 [8192], P(('grid', 'atom'))
Inputs may be any that keep to these rules, and one draw needn't show every extreme that they name: `block_lists`: each row names 4 different blocks; a batch b of group g = b // 8 names only blocks (g - 1) * 12 to (g + 2) * 12 - 1. `point_atoms`: the 256 points of one device name atom centres of one run of max(8, 1) consecutive centres, counted round.
All inputs are finite; a program needn't handle non-finite values.
Results may differ from a plain program's by a relative error of at most 0.04.
Values may be sent and summed in bfloat16 or wider, within the bound.
A program may use at most 128 MiB of HBM per device.

v0:
```python
import jax
import jax.numpy as jnp
from jax import lax
from jax.sharding import PartitionSpec as P

ATOM_DEV = 32


def padded(cells, sides, width):
    for axis, dim in sides:
        count = lax.axis_size(axis)
        ends = count - 1
        head = lax.slice_in_dim(cells, 0, width, axis=dim)
        tail = lax.slice_in_dim(cells, cells.shape[dim] - width, cells.shape[dim], axis=dim)
        cells = jnp.concatenate(
            [
                lax.ppermute(tail, axis, [(i, (i + 1) % count) for i in range(ends)]),
                cells,
                lax.ppermute(head, axis, [((i + 1) % count, i) for i in range(ends)]),
            ],
            axis=dim,
        )
    return cells


def passed_along(value, axis, steps):
    count = lax.axis_size(axis)
    leading, last = (max(0, -steps), min(count, count - steps))
    return lax.ppermute(value, axis, [(source, source + steps) for source in range(leading, last)])


def orbital_values(piece, lists, blocks):
    count = piece.shape[0]
    chosen = blocks[lists].reshape(count, -1, blocks.shape[2])
    values = jnp.einsum("bpk,bko->bpo", piece, chosen, preferred_element_type=jnp.float32)
    return values.astype(jnp.bfloat16)


def fock_terms(piece, lists, psi_rows, scale_rows, total):
    weighted_psi = (scale_rows[:, :, None] * psi_rows.astype(jnp.float32)).astype(jnp.bfloat16)
    terms = jnp.einsum("bpk,bpo->bko", piece, weighted_psi, preferred_element_type=jnp.float32)
    terms = terms.reshape(-1, total.shape[1], total.shape[2])
    return total.at[lists.reshape(-1)].add(terms)


def atom_update(rows, mass, weight):
    mean = rows / (1.0 + mass[:, None])
    return jax.nn.silu(
        jnp.dot(mean.astype(jnp.bfloat16), weight, preferred_element_type=jnp.float32)
    ).astype(jnp.bfloat16)


def local(
    basis_values,
    block_lists,
    orbitals,
    point_weights,
    point_atoms,
    embed_scale,
    embed_shift,
    message_weight,
    atom_weight,
    head_weight,
):
    own_rows = orbitals.shape[0]
    gathered = padded(orbitals, (("grid", 0),), own_rows)
    width = basis_values.shape[2] // block_lists.shape[1]
    owned = own_rows // width
    blocks = gathered.reshape(-1, width, gathered.shape[1])
    offset = (lax.axis_index("grid") - 1) * owned
    local_lists = block_lists - offset
    group_values = lax.all_gather(basis_values, "atom", axis=0, tiled=True)
    psi = orbital_values(group_values, local_lists, blocks)
    squares = 2.0 * jnp.sum(jnp.square(psi.astype(jnp.float32)), axis=2).reshape(-1)
    density = lax.psum_scatter(squares, "atom", scatter_dimension=0, tiled=True)
    radius = jnp.cbrt(density)
    hidden = jax.nn.silu(radius[:, None] * embed_scale[None, :] + embed_shift[None, :])
    atom_total = ATOM_DEV * lax.axis_size("atom")
    onehot = point_atoms[:, None] == jnp.arange(atom_total, dtype=jnp.int32)[None, :]
    selector = onehot.astype(jnp.bfloat16)
    counts = jnp.dot(point_weights, onehot.astype(jnp.float32), precision=lax.Precision.HIGHEST)
    for layer in range(message_weight.shape[0]):
        message = jax.nn.silu(
            jnp.dot(
                hidden.astype(jnp.bfloat16),
                message_weight[layer],
                preferred_element_type=jnp.float32,
            )
        )
        weighted = (point_weights[:, None] * message).astype(jnp.bfloat16)
        partial_value = lax.dot_general(
            selector, weighted, (((0,), (0,)), ((), ())), preferred_element_type=jnp.float32
        )
        rows, mass = (
            lax.psum_scatter(
                partial_value.astype(jnp.bfloat16), "atom", scatter_dimension=0, tiled=True
            ).astype(jnp.float32),
            lax.psum_scatter(
                counts.astype(jnp.bfloat16), "atom", scatter_dimension=0, tiled=True
            ).astype(jnp.float32),
        )
        rows, mass = (
            lax.psum(rows.astype(jnp.bfloat16), "grid").astype(jnp.float32),
            lax.psum(mass.astype(jnp.bfloat16), "grid").astype(jnp.float32),
        )
        update = atom_update(rows, mass, atom_weight[layer])
        features = lax.all_gather(update, "atom", axis=0, tiled=True)
        picked = jnp.dot(selector, features, preferred_element_type=jnp.float32)
        hidden = hidden + message * picked
    score = jnp.dot(hidden, head_weight, precision=lax.Precision.HIGHEST)
    potential = radius * (1.0 + jnp.tanh(score))
    scaled = lax.all_gather(point_weights * potential, "atom", axis=0, tiled=True)
    scaled = scaled.reshape(psi.shape[0], psi.shape[1])
    empty = jnp.zeros((blocks.shape[0], width, psi.shape[2]), jnp.float32)
    total = fock_terms(group_values, local_lists, psi, scaled, empty)
    rounded = lax.optimization_barrier(
        total.reshape(3, own_rows, total.shape[2]).astype(jnp.bfloat16)
    )
    from_below = passed_along(rounded[2], "grid", 1)
    from_above = passed_along(rounded[0], "grid", -1)
    fock_orbitals = (
        rounded[1].astype(jnp.float32)
        + from_below.astype(jnp.float32)
        + from_above.astype(jnp.float32)
    )
    return (fock_orbitals, potential)


def solution(mesh):
    return jax.shard_map(
        local,
        mesh=mesh,
        in_specs=(
            P(("grid", "atom"), None, None),
            P("grid", None),
            P("grid", "atom"),
            P(("grid", "atom")),
            P(("grid", "atom")),
            P(),
            P(),
            P(),
            P(),
            P(),
        ),
        out_specs=(P("grid", "atom"), P(("grid", "atom"))),
        check_vma=False,
    )
```

profile of v0, /device:TPU:1, one launch (start us, length us, event | category | flops | bytes accessed | tf_op | source)
XLA Modules:
  0.0 383.1 jit_solution(17801122140071858288)
XLA Ops:
  7.2 4.5 %collective-permute-start = (bf16[1536,1024]{1,0:T(8,128)(2,1)}, bf16[1536,1024]{1,0:T(8,128)(2,1)S(1)}, u32[]{:S(2)}, u32[]{:S(2)}) collective-permute-start(bf16[1536,1024]{1,0:T(8,128)(2,1)} %param.12), channel_id=1, source_target_pairs={{0,4},{4,8},{8,12},{12,16},{16,20},{20,24},{24,28},{1,5},{5,9},{9,... | collective-permute-start | bytes 9437192 | tf_op jit(solution)/shard_map/ppermute | solution.py:17
  11.7 1.9 collective-permute-start.1
  13.7 0.0 reduce-scatter.3.cloned.1.call-start
  13.7 1.2 dynamic-slice
  16.3 0.7 compare_select_fusion
  17.0 0.1 copy.20
  17.1 0.1 reshape.66
  17.1 0.1 copy.19
  17.2 0.1 reshape.59
  17.3 28.9 %collective-permute-done = bf16[1536,1024]{1,0:T(8,128)(2,1)S(1)} collective-permute-done((bf16[1536,1024]{1,0:T(8,128)(2,1)}, bf16[1536,1024]{1,0:T(8,128)(2,1)S(1)}, u32[]{:S(2)}, u32[]{:S(2)}) %collective-permute-start) | collective-permute-done | bytes 3145760 | tf_op jit(solution)/shard_map/ppermute | solution.py:17
  46.2 35.4 %collective-permute-done.1 = bf16[1536,1024]{1,0:T(8,128)(2,1)} collective-permute-done((bf16[1536,1024]{1,0:T(8,128)(2,1)}, bf16[1536,1024]{1,0:T(8,128)(2,1)}, u32[]{:S(2)}, u32[]{:S(2)}) %collective-permute-start.1) | collective-permute-done | bytes 3145760 | tf_op jit(solution)/shard_map/ppermute | solution.py:19
  81.6 7.0 %pad_maximum_fusion = bf16[4608,1024]{1,0:T(8,128)(2,1)} fusion(bf16[1536,1024]{1,0:T(8,128)(2,1)} %collective-permute-done.1, bf16[1536,1024]{1,0:T(8,128)(2,1)} %param.12, bf16[1536,1024]{1,0:T(8,128)(2,1)S(1)} %collective-permute-done), kind=kLoop, calls=%fused_computation.2 | loop fusion | flops 28311552 | bytes 18874368 | tf_op jit(solution)/shard_map/concatenate | solution.py:15
  88.6 8.8 %gather_fusion = bf16[32,128,1024]{2,1,0:T(8,128)(2,1)} fusion(bf16[36,128,1024]{2,1,0:T(8,128)(2,1)} %bitcast.59, s32[1024]{0:T(1024)S(1)} %pad_clamp_fusion), kind=kCustom, calls=%fused_computation | custom fusion | bytes 16777344 | tf_op jit(solution)/shard_map/gather | solution.py:34
  97.4 6.4 %fusion.1 = (f32[8,128]{1,0:T(8,128)S(1)}, bf16[8,1024,128]{2,1,0:T(8,128)(2,1)S(1)}) fusion(bf16[8,512,1024]{2,1,0:T(8,128)(2,1)} %bitcast.60, bf16[8,128,512]{2,1,0:T(8,128)(2,1)} %all-gather.3.cloned.1.call-done), kind=kOutput, calls=%fused_computation.7 | convolution fusion | flops 1077935104 | bytes 11538432 | tf_op jit(solution)/shard_map/bpk,bko->bpo/dot_general | solution.py:35
  103.8 10.1 %all-reduce = f32[1024]{0:T(1024)S(1)} all-reduce(f32[1024]{0:T(1024)S(1)} %multiply_bitcast_fusion), channel_id=2, replica_groups=mesh['grid'=8,'atom'=4] {'atom'}, use_global_device_ids=true, to_apply=%region_1.0.clone | all-reduce | flops 1024 | bytes 8192
  113.9 0.1 dynamic-slice_cbrt_fusion
  114.0 1.2 divide_multiply_fusion.1
  115.2 0.9 convolution_convert_fusion.2
  116.2 0.0 reduce-scatter.5.cloned.1.call-start
  116.3 0.2 fusion.8
  116.5 6.7 %all-reduce.1 = bf16[128]{0:T(256)(128)(2,1)S(1)} all-reduce(bf16[128]{0:T(256)(128)(2,1)S(1)} %fusion.8), channel_id=4, replica_groups=mesh['grid'=8,'atom'=4] {'atom'}, use_global_device_ids=true, to_apply=%region_4.5.clone | all-reduce | flops 128 | bytes 512
  123.1 0.1 dynamic-slice.3
  123.2 7.5 %reduce-scatter.3.cloned.1.call-done = bf16[32,256]{1,0:T(8,128)(2,1)} async-done(((bf16[128,256]{1,0:T(8,128)(2,1)}), bf16[32,256]{1,0:T(8,128)(2,1)}) %reduce-scatter.3.cloned.1.call-update) | async-done | bytes 16400 | tf_op jit(solution)/shard_map/reduce_scatter | solution.py:95
  130.7 22.6 %all-reduce.2 = (bf16[32,256]{1,0:T(8,128)(2,1)S(1)}, bf16[32]{0:T(256)(128)(2,1)S(1)}) all-reduce(bf16[32,256]{1,0:T(8,128)(2,1)} %reduce-scatter.3.cloned.1.call-done, bf16[32]{0:T(256)(128)(2,1)S(1)} %dynamic-slice.3), channel_id=1, replica_groups=mesh['grid'=8,'atom'=4] {'grid'}, use_global_device_ids=true, to_apply=%region_3.4 | all-reduce | flops 8224 | bytes 32896 | tf_op jit(solution)/shard_map/psum | solution.py:103
  153.4 1.1 multiply_convert_fusion.5
  154.5 10.3 %all_gather.13 = bf16[128,256]{1,0:T(8,128)(2,1)S(1)} all-gather(bf16[32,256]{1,0:T(8,128)(2,1)S(1)} %multiply_convert_fusion.5), channel_id=1, replica_groups=mesh['grid'=8,'atom'=4] {'atom'}, dimensions={0}, use_global_device_ids=true | all-gather | bytes 81920 | tf_op jit(solution)/shard_map/all_gather | solution.py:107
  164.8 0.2 fusion.7
  165.1 0.7 copy-done.3
  165.8 1.1 divide_multiply_fusion
  166.9 0.9 convolution_convert_fusion.1
  167.8 19.8 %reduce-scatter.5.cloned.1.call-done = bf16[32,256]{1,0:T(8,128)(2,1)} async-done(((bf16[128,256]{1,0:T(8,128)(2,1)}), bf16[32,256]{1,0:T(8,128)(2,1)}) %reduce-scatter.5.cloned.1.call-update) | async-done | bytes 16400 | tf_op jit(solution)/shard_map/reduce_scatter | solution.py:95
  187.6 22.6 %psum.26 = bf16[32,256]{1,0:T(8,128)(2,1)S(1)} all-reduce(bf16[32,256]{1,0:T(8,128)(2,1)} %reduce-scatter.5.cloned.1.call-done), channel_id=1, replica_groups=mesh['grid'=8,'atom'=4] {'grid'}, use_global_device_ids=true, to_apply=%region_7.8 | all-reduce | flops 8192 | bytes 32768 | tf_op jit(solution)/shard_map/psum | solution.py:103
  210.2 1.1 multiply_convert_fusion.4
  211.3 10.4 %all_gather.14 = bf16[128,256]{1,0:T(8,128)(2,1)S(1)} all-gather(bf16[32,256]{1,0:T(8,128)(2,1)S(1)} %multiply_convert_fusion.4), channel_id=1, replica_groups=mesh['grid'=8,'atom'=4] {'atom'}, dimensions={0}, use_global_device_ids=true | all-gather | bytes 81920 | tf_op jit(solution)/shard_map/all_gather | solution.py:107
  221.7 1.2 fusion.6
  222.9 0.3 fusion.48
  223.2 0.7 fusion.47
  223.9 6.3 %all-gather = f32[4,1,256]{2,1,0:T(1,128)S(1)} all-gather(f32[1,1,256]{2,1,0:T(1,128)S(1)} %bitcast.64), channel_id=1, replica_groups=mesh['grid'=8,'atom'=4] {'atom'}, dimensions={0}, use_global_device_ids=true | all-gather | bytes 5120 | tf_op jit(solution)/shard_map/all_gather | solution.py:112
  230.2 8.1 %fusion.3 = f32[8,1024,512]{1,2,0:T(8,128)} fusion(bf16[8,128,512]{2,1,0:T(8,128)(2,1)S(1)} %copy-done.2, bf16[8,1024,128]{2,1,0:T(8,128)(2,1)S(1)} %get-tuple-element.11, f32[8,128]{1,0:T(8,128)S(1)} %bitcast.61), kind=kOutput, calls=%fused_computation.12 | convolution fusion | flops 1076887552 | bytes 19927040 | tf_op jit(solution)/shard_map/bpk,bpo->bko/dot_general | solution.py:41
  238.3 8.9 %broadcast_in_dim.4 = f32[36,128,1024]{2,1,0:T(8,128)} broadcast(f32[]{:T(128)} %constant.9.clone.1), dimensions={} | broadcast | bytes 18874372 | tf_op jit(solution)/shard_map/broadcast_in_dim | solution.py:114
  247.2 36.1 %scatter_fusion = f32[36,128,1024]{2,1,0:T(8,128)} fusion(f32[36,128,1024]{2,1,0:T(8,128)} %broadcast_in_dim.4, s32[32]{0:T(128)S(1)} %fusion.45, f32[32,128,1024]{2,1,0:T(8,128)} %bitcast.56), kind=kCustom, calls=%fused_computation.1 | custom fusion | flops 4194304 | bytes 50331776 | tf_op jit(solution)/shard_map/scatter-add | solution.py:43
  283.3 7.1 %convert_element_type.102 = bf16[36,128,1024]{2,1,0:T(8,128)(2,1)S(1)} convert(f32[36,128,1024]{2,1,0:T(8,128)} %scatter_fusion) | non-fusion elementwise | flops 4718592 | bytes 28311552 | tf_op jit(solution)/shard_map/convert_element_type | solution.py:117
  290.4 0.7 slice_bitcast_fusion.1
  291.1 8.8 %collective-permute-start.2 = (bf16[1536,1024]{1,0:T(8,128)(2,1)S(1)}, bf16[1536,1024]{1,0:T(8,128)(2,1)S(1)}, u32[]{:S(2)}, u32[]{:S(2)}) collective-permute-start(bf16[1536,1024]{1,0:T(8,128)(2,1)S(1)} %get-tuple-element.8), channel_id=1, source_target_pairs={{0,4},{4,8},{8,12},{12,16},{16,20},{20,24},{24,28},{1,5},{5,9},{9,... | collective-permute-start | bytes 9437192 | tf_op jit(solution)/shard_map/ppermute | solution.py:29
  299.9 2.8 collective-permute-start.3
  302.7 31.4 %collective-permute-done.2 = bf16[1536,1024]{1,0:T(8,128)(2,1)S(1)} collective-permute-done((bf16[1536,1024]{1,0:T(8,128)(2,1)S(1)}, bf16[1536,1024]{1,0:T(8,128)(2,1)S(1)}, u32[]{:S(2)}, u32[]{:S(2)}) %collective-permute-start.2) | collective-permute-done | bytes 3145760 | tf_op jit(solution)/shard_map/ppermute | solution.py:29
  334.1 37.6 %collective-permute-done.3 = bf16[1536,1024]{1,0:T(8,128)(2,1)S(1)} collective-permute-done((bf16[1536,1024]{1,0:T(8,128)(2,1)S(1)}, bf16[1536,1024]{1,0:T(8,128)(2,1)S(1)}, u32[]{:S(2)}, u32[]{:S(2)}) %collective-permute-start.3) | collective-permute-done | bytes 3145760 | tf_op jit(solution)/shard_map/ppermute | solution.py:29
  371.7 4.9 %fusion = f32[1536,1024]{1,0:T(8,128)} fusion(bf16[1536,1024]{1,0:T(8,128)(2,1)S(1)} %collective-permute-done.3, bf16[1536,1024]{1,0:T(8,128)(2,1)S(1)} %collective-permute-done.2, bf16[3,1536,1024]{2,1,0:T(8,128)(2,1)S(1)} %bitcast.58), kind=kLoop, calls=%fused_computation.4 | loop fusion | flops 7864320 | bytes 15728640 | tf_op jit(solution)/shard_map/add | solution.py:122
  (24 shorter events, 0.2 us)
Async XLA Ops:
  7.2 215.7 %copy-start = (f32[256]{0:T(256)S(1)}, f32[256]{0:T(256)}, u32[]{:S(2)}) copy-start(f32[256]{0:T(256)} %param.19) | copy-start | bytes 3076
  7.2 90.2 %all-gather.3.cloned.1.call-start = ((), (), s32[]{:S(2)}) async-start(), calls=%async_computation.2 | async-start | bytes 1310720 | tf_op jit(solution)/shard_map/all_gather | solution.py:72
  7.2 39.0 %collective-permute-start = (bf16[1536,1024]{1,0:T(8,128)(2,1)}, bf16[1536,1024]{1,0:T(8,128)(2,1)S(1)}, u32[]{:S(2)}, u32[]{:S(2)}) collective-permute-start(bf16[1536,1024]{1,0:T(8,128)(2,1)} %param.12), channel_id=1, source_target_pairs={{0,4},{4,8},{8,12},{12,16},{16,20},{20,24},{24,28},{1,5},{5,9},{9,... | collective-permute-start | bytes 9437192 | tf_op jit(solution)/shard_map/ppermute | solution.py:17
  11.7 69.9 %collective-permute-start.1 = (bf16[1536,1024]{1,0:T(8,128)(2,1)}, bf16[1536,1024]{1,0:T(8,128)(2,1)}, u32[]{:S(2)}, u32[]{:S(2)}) collective-permute-start(bf16[1536,1024]{1,0:T(8,128)(2,1)} %param.12), channel_id=1, source_target_pairs={{4,0},{8,4},{12,8},{16,12},{20,16},{24,20},{28,24},{5,1},{9,5},{13... | collective-permute-start | bytes 9437192 | tf_op jit(solution)/shard_map/ppermute | solution.py:19
  13.7 117.0 %reduce-scatter.3.cloned.1.call-start = ((), (), s32[]{:S(2)}) async-start(), calls=%async_computation.3 | async-start | bytes 81920 | tf_op jit(solution)/shard_map/reduce_scatter | solution.py:95
  97.4 16.6 %copy-start.6 = (f32[256]{0:T(256)S(1)}, f32[256]{0:T(256)}, u32[]{:S(2)}) copy-start(f32[256]{0:T(256)} %param.16) | copy-start | bytes 3076
  97.4 16.6 %copy-start.7 = (f32[256]{0:T(256)S(1)}, f32[256]{0:T(256)}, u32[]{:S(2)}) copy-start(f32[256]{0:T(256)} %param.15) | copy-start | bytes 3076
  97.4 17.9 %copy-start.4 = (s32[256]{0:T(256)S(1)}, s32[256]{0:T(256)}, u32[]{:S(2)}) copy-start(s32[256]{0:T(256)} %param.14) | copy-start | bytes 3076
  97.4 17.9 %copy-start.5 = (f32[256]{0:T(256)S(1)}, f32[256]{0:T(256)}, u32[]{:S(2)}) copy-start(f32[256]{0:T(256)} %param.13) | copy-start | bytes 3076
  103.8 126.4 %copy-start.2 = (bf16[8,128,512]{2,1,0:T(8,128)(2,1)S(1)}, bf16[8,128,512]{2,1,0:T(8,128)(2,1)}, u32[]{:S(2)}) copy-start(bf16[8,128,512]{2,1,0:T(8,128)(2,1)} %all-gather.3.cloned.1.call-done) | copy-start | bytes 3145732
  116.2 71.4 %reduce-scatter.5.cloned.1.call-start = ((), (), s32[]{:S(2)}) async-start(), calls=%async_computation.4 | async-start | bytes 81920 | tf_op jit(solution)/shard_map/reduce_scatter | solution.py:95
  165.0 0.7 copy-start.3
  291.1 43.0 %collective-permute-start.2 = (bf16[1536,1024]{1,0:T(8,128)(2,1)S(1)}, bf16[1536,1024]{1,0:T(8,128)(2,1)S(1)}, u32[]{:S(2)}, u32[]{:S(2)}) collective-permute-start(bf16[1536,1024]{1,0:T(8,128)(2,1)S(1)} %get-tuple-element.8), channel_id=1, source_target_pairs={{0,4},{4,8},{8,12},{12,16},{16,20},{20,24},{24,28},{1,5},{5,9},{9,... | collective-permute-start | bytes 9437192 | tf_op jit(solution)/shard_map/ppermute | solution.py:29
  299.9 76.7 %copy-start.1 = (f32[256]{0:T(256)S(1)}, f32[256]{0:T(256)}, u32[]{:S(2)}) copy-start(f32[256]{0:T(256)} %param.19) | copy-start | bytes 3076
  299.9 71.7 %collective-permute-start.3 = (bf16[1536,1024]{1,0:T(8,128)(2,1)S(1)}, bf16[1536,1024]{1,0:T(8,128)(2,1)S(1)}, u32[]{:S(2)}, u32[]{:S(2)}) collective-permute-start(bf16[1536,1024]{1,0:T(8,128)(2,1)S(1)} %get-tuple-element.9), channel_id=1, source_target_pairs={{4,0},{8,4},{12,8},{16,12},{20,16},{24,20},{28,24},{5,1},{9,5},{13... | collective-permute-start | bytes 9437192 | tf_op jit(solution)/shard_map/ppermute | solution.py:29
Sparse Core Ops, SparseCore 0:
  13.8 28.7 all-gather.2
  116.3 14.3 reduce-scatter.2
  168.0 19.5 reduce-scatter.4
where the time goes:
time: 384 us; the launch traced here: 383 us
  waiting for transfers between devices  161 us (42%)
  blocking collectives  89 us (23%)
  other arithmetic  56.6 us (15%)
  matrix products  22.9 us (6%)
  local copies, waits for them, and re-layouts  20.8 us (5%)
  starting transfers between devices  18.1 us (5%)
  between operations  15.3 us (4%)
    ppermute x2, waiting for transfers between devices, passed_along(): lax.ppermute(value, axis, [(source, source + steps) for source in range(l...  69 us
    psum x2, blocking collectives, local(): lax.psum(rows.astype(jnp.bfloat16), 'grid').astype(jnp.float32)  45.2 us
    scatter-add x1, other arithmetic, fock_terms(): return total.at[lists.reshape(-1)].add(terms)  36.1 us
    ppermute x1, waiting for transfers between devices, padded(): lax.ppermute(head, axis, [((i + 1) % count, i) for i in range(ends)])  35.4 us
    ppermute x1, waiting for transfers between devices, padded(): lax.ppermute(tail, axis, [(i, (i + 1) % count) for i in range(ends)])  28.9 us
    reduce_scatter x2, waiting for transfers between devices, local(): lax.psum_scatter(partial_value.astype(jnp.bfloat16), 'atom', scatter_dime...  27.3 us
    all_gather x2, blocking collectives, local(): features = lax.all_gather(update, 'atom', axis=0, tiled=True)  20.7 us
    unnamed x2, blocking collectives  16.8 us
  transfers between devices with their start and end apart: 7, of which 6 were waited for; matrix products, arithmetic and copies ran while one was open for 5% of the time, Pallas kernels for 0%

commit v1 on v0

--- a/solution.py
+++ b/solution.py
@@ -100,7 +100,7 @@
             ).astype(jnp.float32),
         )
         rows, mass = (
-            lax.psum(rows.astype(jnp.bfloat16), "grid").astype(jnp.float32),
+            jnp.sum(lax.all_gather(rows.astype(jnp.bfloat16), "grid"), axis=0).astype(jnp.float32),
             lax.psum(mass.astype(jnp.bfloat16), "grid").astype(jnp.float32),
         )
         update = atom_update(rows, mass, atom_weight[layer])

time: 384 us -> 369 us (0.961)
  waiting for transfers between devices: 161 us -> 102 us
  blocking collectives: 89 us -> 131 us
    ppermute x1, waiting for transfers between devices: 35.4 us -> 0.01 us  [padded(): lax.ppermute(head, axis, [((i + 1) % count, i) for i in range(ends)])]
    ppermute x1, waiting for transfers between devices: 28.9 us -> 0.01 us  [padded(): lax.ppermute(tail, axis, [(i, (i + 1) % count) for i in range(ends)])]
    all_gather x0 -> x2, blocking collectives: none -> 24.2 us  [local(): lax.all_gather(rows.astype(jnp.bfloat16), 'grid')]
    psum x2 -> x1, blocking collectives: 45.2 us -> 60.2 us  [local(): lax.psum(mass.astype(jnp.bfloat16), 'grid').astype(jnp.float32)]
    reduce_scatter x2, waiting for transfers between devices: 27.3 us -> 34.8 us  [local(): lax.psum_scatter(partial_value.astype(jnp.bfloat16), 'atom', scatter_dime...]
  transfers between devices with their start and end apart: 7 -> 7, of which waited for: 6 -> 4; matrix products, arithmetic and copies ran while one was open for 5% -> 5% of each run, Pallas kernels for 0% -> 0%
where the time goes in v1:
time: 369 us
  blocking collectives  131 us (36%)
  waiting for transfers between devices  102 us (28%)
  other arithmetic  57.8 us (16%)
  matrix products  24.5 us (7%)
  local copies, waits for them, and re-layouts  20.9 us (6%)
  starting transfers between devices  16.4 us (4%)
  between operations  15.3 us (4%)
    ppermute x2, waiting for transfers between devices, passed_along(): lax.ppermute(value, axis, [(source, source + steps) for source in range(l...  67.4 us
    psum x1, blocking collectives, local(): lax.psum(mass.astype(jnp.bfloat16), 'grid').astype(jnp.float32)  60.2 us
    scatter-add x1, other arithmetic, fock_terms(): return total.at[lists.reshape(-1)].add(terms)  36.1 us
    reduce_scatter x2, waiting for transfers between devices, local(): lax.psum_scatter(partial_value.astype(jnp.bfloat16), 'atom', scatter_dime...  34.8 us
    all_gather x2, blocking collectives, local(): lax.all_gather(rows.astype(jnp.bfloat16), 'grid')  24.2 us
    all_gather x2, blocking collectives, local(): features = lax.all_gather(update, 'atom', axis=0, tiled=True)  20.5 us
    unnamed x2, blocking collectives  20.1 us
    ppermute x2, starting transfers between devices, passed_along(): lax.ppermute(value, axis, [(source, source + steps) for source in range(l...  9.89 us
  transfers between devices with their start and end apart: 7, of which 4 were waited for; matrix products, arithmetic and copies ran while one was open for 5% of the time, Pallas kernels for 0%

profile of v1, /device:TPU:1, one launch (start us, length us, event | category | flops | bytes accessed | tf_op | source)
XLA Modules:
  0.0 368.6 jit_solution(11819360222534287462)
XLA Ops:
  7.2 4.5 %collective-permute-start = (bf16[1536,1024]{1,0:T(8,128)(2,1)}, bf16[1536,1024]{1,0:T(8,128)(2,1)S(1)}, u32[]{:S(2)}, u32[]{:S(2)}) collective-permute-start(bf16[1536,1024]{1,0:T(8,128)(2,1)} %param.12), channel_id=1, source_target_pairs={{0,4},{4,8},{8,12},{12,16},{16,20},{20,24},{24,28},{1,5},{5,9},{9,... | collective-permute-start | bytes 9437192 | tf_op jit(solution)/shard_map/ppermute | solution.py:17
  11.7 1.9 collective-permute-start.1
  13.7 0.0 reduce-scatter.3.cloned.1.call-start
  13.7 1.2 dynamic-slice
  15.6 0.9 fusion.8
  16.6 10.0 %all-reduce.1 = bf16[128]{0:T(256)(128)(2,1)S(1)} all-reduce(bf16[128]{0:T(256)(128)(2,1)S(1)} %fusion.8), channel_id=6, replica_groups=mesh['grid'=8,'atom'=4] {'atom'}, use_global_device_ids=true, to_apply=%region_4.5.clone | all-reduce | flops 128 | bytes 512
  26.6 0.1 dynamic-slice.3
  26.7 60.2 %psum.6 = bf16[32]{0:T(256)(128)(2,1)S(1)} all-reduce(bf16[32]{0:T(256)(128)(2,1)S(1)} %dynamic-slice.3), channel_id=1, replica_groups=mesh['grid'=8,'atom'=4] {'grid'}, use_global_device_ids=true, to_apply=%region_5.6 | all-reduce | flops 32 | bytes 128 | tf_op jit(solution)/shard_map/psum | solution.py:104
  87.6 0.7 compare_select_fusion
  88.3 0.1 copy.20
  88.3 0.1 reshape.66
  88.4 0.1 copy.19
  88.5 0.1 reshape.59
  88.6 7.0 %pad_maximum_fusion = bf16[4608,1024]{1,0:T(8,128)(2,1)} fusion(bf16[1536,1024]{1,0:T(8,128)(2,1)} %collective-permute-done.1, bf16[1536,1024]{1,0:T(8,128)(2,1)} %param.12, bf16[1536,1024]{1,0:T(8,128)(2,1)S(1)} %collective-permute-done), kind=kLoop, calls=%fused_computation.2 | loop fusion | flops 28311552 | bytes 18874368 | tf_op jit(solution)/shard_map/concatenate | solution.py:15
  95.6 8.8 %gather_fusion = bf16[32,128,1024]{2,1,0:T(8,128)(2,1)} fusion(bf16[36,128,1024]{2,1,0:T(8,128)(2,1)} %bitcast.61, s32[1024]{0:T(1024)S(1)} %pad_clamp_fusion), kind=kCustom, calls=%fused_computation | custom fusion | bytes 16777344 | tf_op jit(solution)/shard_map/gather | solution.py:34
  104.4 6.4 %fusion.1 = (f32[8,128]{1,0:T(8,128)S(1)}, bf16[8,1024,128]{2,1,0:T(8,128)(2,1)S(1)}) fusion(bf16[8,512,1024]{2,1,0:T(8,128)(2,1)} %bitcast.62, bf16[8,128,512]{2,1,0:T(8,128)(2,1)} %all-gather.5.cloned.1.call-done), kind=kOutput, calls=%fused_computation.7 | convolution fusion | flops 1077935104 | bytes 11538432 | tf_op jit(solution)/shard_map/bpk,bko->bpo/dot_general | solution.py:35
  110.9 10.1 %all-reduce = f32[1024]{0:T(1024)S(1)} all-reduce(f32[1024]{0:T(1024)S(1)} %multiply_bitcast_fusion), channel_id=4, replica_groups=mesh['grid'=8,'atom'=4] {'atom'}, use_global_device_ids=true, to_apply=%region_1.0.clone | all-reduce | flops 1024 | bytes 8192
  120.9 0.1 dynamic-slice_cbrt_fusion
  121.0 1.2 divide_multiply_fusion.1
  122.3 0.9 convolution_convert_fusion.2
  123.3 18.6 %reduce-scatter.3.cloned.1.call-done = bf16[32,256]{1,0:T(8,128)(2,1)} async-done(((bf16[128,256]{1,0:T(8,128)(2,1)}), bf16[32,256]{1,0:T(8,128)(2,1)}) %reduce-scatter.3.cloned.1.call-update) | async-done | bytes 16400 | tf_op jit(solution)/shard_map/reduce_scatter | solution.py:95
  141.9 12.1 %all-gather = bf16[256,256]{1,0:T(8,128)(2,1)S(1)} all-gather(bf16[32,256]{1,0:T(8,128)(2,1)} %reduce-scatter.3.cloned.1.call-done), channel_id=2, replica_groups=mesh['grid'=8,'atom'=4] {'grid'}, dimensions={0}, use_global_device_ids=true | all-gather | bytes 147456 | tf_op jit(solution)/shard_map/all_gather | solution.py:103
  154.1 1.1 multiply_convert_fusion.5
  155.2 10.2 %all_gather.27 = bf16[128,256]{1,0:T(8,128)(2,1)S(1)} all-gather(bf16[32,256]{1,0:T(8,128)(2,1)S(1)} %multiply_convert_fusion.5), channel_id=1, replica_groups=mesh['grid'=8,'atom'=4] {'atom'}, dimensions={0}, use_global_device_ids=true | all-gather | bytes 81920 | tf_op jit(solution)/shard_map/all_gather | solution.py:107
  165.4 1.2 fusion.7
  166.6 0.7 copy-done.4
  167.3 1.1 divide_multiply_fusion
  168.4 0.9 convolution_convert_fusion.1
  169.4 0.5 fusion.45
  169.9 16.2 %reduce-scatter.5.cloned.1.call-done = bf16[32,256]{1,0:T(8,128)(2,1)} async-done(((bf16[128,256]{1,0:T(8,128)(2,1)}), bf16[32,256]{1,0:T(8,128)(2,1)}) %reduce-scatter.5.cloned.1.call-update) | async-done | bytes 16400 | tf_op jit(solution)/shard_map/reduce_scatter | solution.py:95
  186.2 12.1 %all-gather.1 = bf16[256,256]{1,0:T(8,128)(2,1)S(1)} all-gather(bf16[32,256]{1,0:T(8,128)(2,1)} %reduce-scatter.5.cloned.1.call-done), channel_id=3, replica_groups=mesh['grid'=8,'atom'=4] {'grid'}, dimensions={0}, use_global_device_ids=true | all-gather | bytes 147456 | tf_op jit(solution)/shard_map/all_gather | solution.py:103
  198.2 0.6 reduce_sum.35
  198.9 1.1 multiply_convert_fusion.4
  200.0 10.2 %all_gather.30 = bf16[128,256]{1,0:T(8,128)(2,1)S(1)} all-gather(bf16[32,256]{1,0:T(8,128)(2,1)S(1)} %multiply_convert_fusion.4), channel_id=1, replica_groups=mesh['grid'=8,'atom'=4] {'atom'}, dimensions={0}, use_global_device_ids=true | all-gather | bytes 81920 | tf_op jit(solution)/shard_map/all_gather | solution.py:107
  210.3 1.2 fusion.6
  211.4 0.3 fusion.48
  211.7 0.7 fusion.47
  212.4 6.4 %all-gather.2 = f32[4,1,256]{2,1,0:T(1,128)S(1)} all-gather(f32[1,1,256]{2,1,0:T(1,128)S(1)} %bitcast.68), channel_id=1, replica_groups=mesh['grid'=8,'atom'=4] {'atom'}, dimensions={0}, use_global_device_ids=true | all-gather | bytes 5120 | tf_op jit(solution)/shard_map/all_gather | solution.py:112
  218.8 8.1 %fusion.3 = f32[8,1024,512]{1,2,0:T(8,128)} fusion(bf16[8,128,512]{2,1,0:T(8,128)(2,1)S(1)} %copy-done.2, bf16[8,1024,128]{2,1,0:T(8,128)(2,1)S(1)} %get-tuple-element.9, f32[8,128]{1,0:T(8,128)S(1)} %bitcast.65), kind=kOutput, calls=%fused_computation.12 | convolution fusion | flops 1076887552 | bytes 19927040 | tf_op jit(solution)/shard_map/bpk,bpo->bko/dot_general | solution.py:41
  227.0 8.9 %broadcast_in_dim.4 = f32[36,128,1024]{2,1,0:T(8,128)} broadcast(f32[]{:T(128)} %constant.10.clone.1), dimensions={} | broadcast | bytes 18874372 | tf_op jit(solution)/shard_map/broadcast_in_dim | solution.py:114
  235.9 36.1 %scatter_fusion = f32[36,128,1024]{2,1,0:T(8,128)} fusion(f32[36,128,1024]{2,1,0:T(8,128)} %broadcast_in_dim.4, s32[32]{0:T(128)S(1)} %copy-done.7, f32[32,128,1024]{2,1,0:T(8,128)} %bitcast.58), kind=kCustom, calls=%fused_computation.1 | custom fusion | flops 4194304 | bytes 50331776 | tf_op jit(solution)/shard_map/scatter-add | solution.py:43
  272.0 7.1 %convert_element_type.106 = bf16[36,128,1024]{2,1,0:T(8,128)(2,1)S(1)} convert(f32[36,128,1024]{2,1,0:T(8,128)} %scatter_fusion) | non-fusion elementwise | flops 4718592 | bytes 28311552 | tf_op jit(solution)/shard_map/convert_element_type | solution.py:117
  279.1 0.7 slice_bitcast_fusion.1
  279.8 8.0 %collective-permute-start.2 = (bf16[1536,1024]{1,0:T(8,128)(2,1)S(1)}, bf16[1536,1024]{1,0:T(8,128)(2,1)S(1)}, u32[]{:S(2)}, u32[]{:S(2)}) collective-permute-start(bf16[1536,1024]{1,0:T(8,128)(2,1)S(1)} %get-tuple-element.6), channel_id=1, source_target_pairs={{0,4},{4,8},{8,12},{12,16},{16,20},{20,24},{24,28},{1,5},{5,9},{9,... | collective-permute-start | bytes 9437192 | tf_op jit(solution)/shard_map/ppermute | solution.py:29
  287.8 1.9 collective-permute-start.3
  289.8 32.3 %collective-permute-done.2 = bf16[1536,1024]{1,0:T(8,128)(2,1)S(1)} collective-permute-done((bf16[1536,1024]{1,0:T(8,128)(2,1)S(1)}, bf16[1536,1024]{1,0:T(8,128)(2,1)S(1)}, u32[]{:S(2)}, u32[]{:S(2)}) %collective-permute-start.2) | collective-permute-done | bytes 3145760 | tf_op jit(solution)/shard_map/ppermute | solution.py:29
  322.0 35.1 %collective-permute-done.3 = bf16[1536,1024]{1,0:T(8,128)(2,1)S(1)} collective-permute-done((bf16[1536,1024]{1,0:T(8,128)(2,1)S(1)}, bf16[1536,1024]{1,0:T(8,128)(2,1)S(1)}, u32[]{:S(2)}, u32[]{:S(2)}) %collective-permute-start.3) | collective-permute-done | bytes 3145760 | tf_op jit(solution)/shard_map/ppermute | solution.py:29
  357.1 4.9 %fusion = f32[1536,1024]{1,0:T(8,128)} fusion(bf16[1536,1024]{1,0:T(8,128)(2,1)S(1)} %collective-permute-done.3, bf16[1536,1024]{1,0:T(8,128)(2,1)S(1)} %collective-permute-done.2, bf16[3,1536,1024]{2,1,0:T(8,128)(2,1)S(1)} %bitcast.60), kind=kLoop, calls=%fused_computation.4 | loop fusion | flops 7864320 | bytes 15728640 | tf_op jit(solution)/shard_map/add | solution.py:122
  (33 shorter events, 0.2 us)
Async XLA Ops:
  7.2 204.3 %copy-start = (f32[256]{0:T(256)S(1)}, f32[256]{0:T(256)}, u32[]{:S(2)}) copy-start(f32[256]{0:T(256)} %param.19) | copy-start | bytes 3076
  7.2 97.2 %all-gather.5.cloned.1.call-start = ((), (), s32[]{:S(2)}) async-start(), calls=%async_computation.2 | async-start | bytes 1310720 | tf_op jit(solution)/shard_map/all_gather | solution.py:72
  7.2 81.4 %collective-permute-start = (bf16[1536,1024]{1,0:T(8,128)(2,1)}, bf16[1536,1024]{1,0:T(8,128)(2,1)S(1)}, u32[]{:S(2)}, u32[]{:S(2)}) collective-permute-start(bf16[1536,1024]{1,0:T(8,128)(2,1)} %param.12), channel_id=1, source_target_pairs={{0,4},{4,8},{8,12},{12,16},{16,20},{20,24},{24,28},{1,5},{5,9},{9,... | collective-permute-start | bytes 9437192 | tf_op jit(solution)/shard_map/ppermute | solution.py:17
  11.7 76.9 %collective-permute-start.1 = (bf16[1536,1024]{1,0:T(8,128)(2,1)}, bf16[1536,1024]{1,0:T(8,128)(2,1)}, u32[]{:S(2)}, u32[]{:S(2)}) collective-permute-start(bf16[1536,1024]{1,0:T(8,128)(2,1)} %param.12), channel_id=1, source_target_pairs={{4,0},{8,4},{12,8},{16,12},{20,16},{24,20},{28,24},{5,1},{9,5},{13... | collective-permute-start | bytes 9437192 | tf_op jit(solution)/shard_map/ppermute | solution.py:19
  13.7 128.2 %reduce-scatter.3.cloned.1.call-start = ((), (), s32[]{:S(2)}) async-start(), calls=%async_computation.3 | async-start | bytes 81920 | tf_op jit(solution)/shard_map/reduce_scatter | solution.py:95
  104.4 16.6 %copy-start.8 = (f32[256]{0:T(256)S(1)}, f32[256]{0:T(256)}, u32[]{:S(2)}) copy-start(f32[256]{0:T(256)} %param.16) | copy-start | bytes 3076
  104.4 16.6 %copy-start.9 = (f32[256]{0:T(256)S(1)}, f32[256]{0:T(256)}, u32[]{:S(2)}) copy-start(f32[256]{0:T(256)} %param.15) | copy-start | bytes 3076
  104.4 17.9 %copy-start.5 = (s32[256]{0:T(256)S(1)}, s32[256]{0:T(256)}, u32[]{:S(2)}) copy-start(s32[256]{0:T(256)} %param.14) | copy-start | bytes 3076
  104.4 17.9 %copy-start.6 = (f32[256]{0:T(256)S(1)}, f32[256]{0:T(256)}, u32[]{:S(2)}) copy-start(f32[256]{0:T(256)} %param.13) | copy-start | bytes 3076
  110.8 108.0 %copy-start.2 = (bf16[8,128,512]{2,1,0:T(8,128)(2,1)S(1)}, bf16[8,128,512]{2,1,0:T(8,128)(2,1)}, u32[]{:S(2)}) copy-start(bf16[8,128,512]{2,1,0:T(8,128)(2,1)} %all-gather.5.cloned.1.call-done) | copy-start | bytes 3145732
  122.3 1.0 copy-start.3
  123.2 62.9 %reduce-scatter.5.cloned.1.call-start = ((), (), s32[]{:S(2)}) async-start(), calls=%async_computation.4 | async-start | bytes 81920 | tf_op jit(solution)/shard_map/reduce_scatter | solution.py:95
  123.3 46.6 %copy-start.10 = (f32[32]{0:T(128)}, f32[32]{0:T(128)S(1)}, u32[]{:S(2)}) copy-start(f32[32]{0:T(128)S(1)} %convert_add_fusion.1) | copy-start | bytes 388
  166.6 0.7 copy-start.4
  227.0 8.9 %copy-start.7 = (s32[32]{0:T(128)S(1)}, s32[32]{0:T(128)}, u32[]{:S(2)}) copy-start(s32[32]{0:T(128)} %fusion.45) | copy-start | bytes 388
  279.8 42.2 %collective-permute-start.2 = (bf16[1536,1024]{1,0:T(8,128)(2,1)S(1)}, bf16[1536,1024]{1,0:T(8,128)(2,1)S(1)}, u32[]{:S(2)}, u32[]{:S(2)}) collective-permute-start(bf16[1536,1024]{1,0:T(8,128)(2,1)S(1)} %get-tuple-element.6), channel_id=1, source_target_pairs={{0,4},{4,8},{8,12},{12,16},{16,20},{20,24},{24,28},{1,5},{5,9},{9,... | collective-permute-start | bytes 9437192 | tf_op jit(solution)/shard_map/ppermute | solution.py:29
  287.8 74.2 %copy-start.1 = (f32[256]{0:T(256)S(1)}, f32[256]{0:T(256)}, u32[]{:S(2)}) copy-start(f32[256]{0:T(256)} %param.19) | copy-start | bytes 3076
  287.8 69.3 %collective-permute-start.3 = (bf16[1536,1024]{1,0:T(8,128)(2,1)S(1)}, bf16[1536,1024]{1,0:T(8,128)(2,1)S(1)}, u32[]{:S(2)}, u32[]{:S(2)}) collective-permute-start(bf16[1536,1024]{1,0:T(8,128)(2,1)S(1)} %get-tuple-element.7), channel_id=1, source_target_pairs={{4,0},{8,4},{12,8},{16,12},{20,16},{24,20},{28,24},{5,1},{9,5},{13... | collective-permute-start | bytes 9437192 | tf_op jit(solution)/shard_map/ppermute | solution.py:29
Sparse Core Ops, SparseCore 0:
  13.8 28.9 all-gather.4
  123.4 18.5 reduce-scatter.2
  169.5 16.6 reduce-scatter.4
